TPU v7x, 128 devices: a whole 4x4x4 slice. The times are simulated.
128 devices in a mesh: leaf: 32 (over x, y, core), nbr: 4 (over z).
Axes of the slice: x: 4, y: 4, z: 4, core: 2. Of those that a mesh axis runs over, the one named last changes fastest.
Arguments:
- points: bfloat16 [1024, 32, 512], P('leaf'), may hold values from -1.1953125 to 1.1953125
- charges: bfloat16 [1024, 64, 512], P('leaf'), may hold values from -1.5 to 1.5
- projection: bfloat16 [1024, 256, 512], P('leaf', 'nbr'), may hold values from -0.25 to 0.25
- skeleton_index: int32 [1024, 256], P('leaf'), may hold values from 0 to 511, as said below
- near_ids: int32 [1024, 8], P('leaf', 'nbr'), may hold values from 0 to 1023, as said below
- far_ids: int32 [1024, 16], P('leaf', 'nbr'), may hold values from 0 to 1023, as said below
Outputs:
- potentials: float32 [1024, 64, 512], P('leaf', None, 'nbr')
Inputs may be any that keep to these rules, and one draw needn't show every extreme that they name: `skeleton_index`: each row holds 256 different point numbers of its leaf. `near_ids`: take the rows of one block of 32 leaves (leaf numbers k * 32 to k * 32 + 31) and one of the 4 equal groups of columns: at most 3 of its entries name leaves of any one such block, and some block is named exactly 3 times. `far_ids`: take the rows of one block of 32 leaves and one of the 4 equal groups of columns: at most 5 of its entries name leaves of any one such block, and some block is named exactly 5 times.
All inputs are finite; a program needn't handle non-finite values.
Results may differ from a plain program's by a relative error of at most 0.002.
Values may be sent and summed in bfloat16 or wider, within the bound.
A program may use at most 128 MiB of HBM per device.

v0:
```python
import math
import jax
import jax.numpy as jnp
from jax import lax
from jax.sharding import PartitionSpec as P

GAMMA = 1.0


def kernel_terms(targets, sources, weights):
    target_f32 = targets.astype(jnp.float32)
    source_f32 = sources.astype(jnp.float32)
    inner_terms = jnp.einsum("dt,dm->tm", targets, sources, preferred_element_type=jnp.float32)
    distance = (
        jnp.sum(target_f32 * target_f32, axis=0)[:, None]
        + jnp.sum(source_f32 * source_f32, axis=0)[None, :]
        - 2.0 * inner_terms
    )
    kernel = jnp.exp(-GAMMA * distance)
    return jnp.einsum(
        "rm,tm->rt",
        weights.astype(jnp.float32),
        kernel,
        precision=lax.Precision.HIGHEST,
        preferred_element_type=jnp.float32,
    )


def group_terms(targets, sources, weights):
    item_count = targets.shape[0]
    column_count = sources.shape[2]
    block_rows = math.gcd(item_count, max(1, 8192 // column_count))
    steps_count = item_count // block_rows

    def run_block(batch_rows):
        return jax.vmap(kernel_terms)(batch_rows[0], batch_rows[1], batch_rows[2])

    stacked = (
        targets.reshape((steps_count, block_rows) + targets.shape[1:]),
        sources.reshape((steps_count, block_rows) + sources.shape[1:]),
        weights.reshape((steps_count, block_rows) + weights.shape[1:]),
    )
    result = lax.map(run_block, stacked)
    return result.reshape((item_count,) + result.shape[2:])


def slot_plan(id_block, capacity, groups, leaf_dev):
    flat_ids = id_block.reshape(-1)
    owners = flat_ids // leaf_dev
    local_leaf = flat_ids % leaf_dev
    member = (owners[:, None] == jnp.arange(groups, dtype=jnp.int32)[None, :]).astype(jnp.int32)
    before = jnp.cumsum(member, axis=0) - member
    rank_slot = jnp.sum(before * member, axis=1)
    return (local_leaf, owners * capacity + rank_slot)


def slot_table(values, slot_ids, capacity, groups):
    matches = slot_ids[:, None] == jnp.arange(groups * capacity, dtype=jnp.int32)[None, :]
    return jnp.sum(jnp.where(matches, values[:, None], 0), axis=0).reshape(groups, capacity)


def gather_entries(received, slot_ids, leaf_dev):
    flat_rows = received.reshape((-1,) + received.shape[2:])
    picked = flat_rows[slot_ids]
    per_target = slot_ids.shape[0] // leaf_dev
    picked = picked.reshape(leaf_dev, per_target, picked.shape[1], picked.shape[2])
    return picked.transpose(0, 2, 1, 3).reshape(
        leaf_dev, picked.shape[2], per_target * picked.shape[3]
    )


def per_device(points, charges, projection, skeleton_index, near_ids, far_ids):
    leaf_dev = points.shape[0]
    groups = lax.axis_size("leaf")
    near_dev = near_ids.shape[1]
    far_dev = far_ids.shape[1]
    cap_near = max(2, (5 * leaf_dev * near_dev + 4 * groups - 1) // (4 * groups))
    cap_far = max(2, (5 * leaf_dev * far_dev + 4 * groups - 1) // (4 * groups))
    partial_value = jnp.einsum(
        "lrp,lsp->lrs", charges, projection, preferred_element_type=jnp.float32
    ).astype(jnp.bfloat16)
    skeleton_charges = lax.all_gather(partial_value, "nbr", axis=2, tiled=True)
    skeleton_points = jnp.take_along_axis(points, skeleton_index[:, None, :], axis=2)
    near_local, near_slots = slot_plan(near_ids, cap_near, groups, leaf_dev)
    far_local, far_slots = slot_plan(far_ids, cap_far, groups, leaf_dev)
    near_table = slot_table(near_local, near_slots, cap_near, groups)
    far_table = slot_table(far_local, far_slots, cap_far, groups)
    near_wanted, far_wanted = (
        lax.all_to_all(near_table, "leaf", split_axis=0, concat_axis=0, tiled=True),
        lax.all_to_all(far_table, "leaf", split_axis=0, concat_axis=0, tiled=True),
    )
    near_points, near_weights, far_points, far_weights = (
        lax.all_to_all(points[near_wanted], "leaf", split_axis=0, concat_axis=0, tiled=True),
        lax.all_to_all(charges[near_wanted], "leaf", split_axis=0, concat_axis=0, tiled=True),
        lax.all_to_all(
            skeleton_points[far_wanted], "leaf", split_axis=0, concat_axis=0, tiled=True
        ),
        lax.all_to_all(
            skeleton_charges[far_wanted], "leaf", split_axis=0, concat_axis=0, tiled=True
        ),
    )
    sources = jnp.concatenate(
        [
            gather_entries(near_points, near_slots, leaf_dev),
            gather_entries(far_points, far_slots, leaf_dev),
        ],
        axis=2,
    )
    weights = jnp.concatenate(
        [
            gather_entries(near_weights, near_slots, leaf_dev),
            gather_entries(far_weights, far_slots, leaf_dev),
        ],
        axis=2,
    )
    terms = group_terms(points, sources, weights)
    return lax.psum_scatter(terms, "nbr", scatter_dimension=2, tiled=True)


def solution(mesh):
    in_specs = (
        P("leaf", None, None),
        P("leaf", None, None),
        P("leaf", "nbr", None),
        P("leaf", None),
        P("leaf", "nbr"),
        P("leaf", "nbr"),
    )
    out_specs = P("leaf", None, "nbr")
    return jax.shard_map(
        per_device, mesh=mesh, in_specs=in_specs, out_specs=out_specs, check_vma=False
    )
```

profile of v0, /device:TPU:1, one launch (start us, length us, event | category | flops | bytes accessed | tf_op | source)
XLA Modules:
  0.0 669.3 jit_solution(7180529218226698054)
XLA Ops:
  8.9 8.6 %all-to-all-start.2 = ((s32[32,1,5]{2,1,0:T(1,128)}), s32[32,1,5]{2,1,0:T(1,128)S(1)}, u32[]{:S(2)}, u32[]{:S(2)}) async-start(s32[32,1,5]{2,1,0:T(1,128)} %bitcast.12), calls=%async_computation.2 | async-start | bytes 32768 | tf_op jit(solution)/shard_map/all_to_all | solution.py:90
  24.9 132.5 %gather_fusion.8 = bf16[8192,32]{1,0:T(8,128)(2,1)} fusion(bf16[32,32,512]{1,2,0:T(8,128)(2,1)} %copy.77, s32[8192]{0:T(1024)S(1)} %bitcast.83), kind=kCustom, calls=%fused_computation.8 | custom fusion | bytes 1114112 | tf_op jit(solution)/shard_map/jit(take_along_axis)/gather | solution.py:83
  162.6 7.3 %all-to-all-start = ((s32[32,1,3]{2,1,0:T(1,128)}), s32[32,1,3]{2,1,0:T(1,128)S(1)}, u32[]{:S(2)}, u32[]{:S(2)}) async-start(s32[32,1,3]{2,1,0:T(1,128)} %bitcast.4), calls=%async_computation | async-start | bytes 32768 | tf_op jit(solution)/shard_map/all_to_all | solution.py:89
  170.0 9.2 %gather_fusion.6 = bf16[160,32,256]{1,2,0:T(8,128)(2,1)} fusion(bf16[32,32,256]{1,2,0:T(8,128)(2,1)} %select_bitcast_fusion, s32[1024]{0:T(1024)S(1)} %pad_clamp_fusion.1), kind=kCustom, calls=%fused_computation.6 | custom fusion | bytes 5243520 | tf_op jit(solution)/shard_map/gather | solution.py:96
  179.1 9.8 %copy.78 = bf16[32,5,32,256]{3,2,1,0:T(8,128)(2,1)} copy(bf16[32,5,32,256]{2,3,1,0:T(8,128)(2,1)} %bitcast.89) | data formatting | bytes 5242880 | tf_op jit(solution)/shard_map/gather | solution.py:96
  188.9 7.6 %all-to-all-start.5 = ((bf16[32,5,32,256]{3,2,1,0:T(8,128)(2,1)}), bf16[32,5,32,256]{3,2,1,0:T(8,128)(2,1)}, u32[]{:S(2)}, u32[]{:S(2)}) async-start(bf16[32,5,32,256]{3,2,1,0:T(8,128)(2,1)} %copy.78), calls=%async_computation.5 | async-start | bytes 5242880 | tf_op jit(solution)/shard_map/all_to_all | solution.py:95
  199.4 31.1 %all-to-all-done.5 = bf16[32,5,32,256]{3,2,1,0:T(8,128)(2,1)} async-done(((bf16[32,5,32,256]{3,2,1,0:T(8,128)(2,1)}), bf16[32,5,32,256]{3,2,1,0:T(8,128)(2,1)}, u32[]{:S(2)}, u32[]{:S(2)}) %all-to-all-start.5) | async-done | bytes 2621472 | tf_op jit(solution)/shard_map/all_to_all | solution.py:95
  230.5 5.3 all-to-all-start.4
  235.8 6.0 gather_fusion
  241.8 33.9 %all-to-all-done.4 = bf16[32,3,32,512]{3,2,1,0:T(8,128)(2,1)} async-done(((bf16[32,3,32,512]{3,2,1,0:T(8,128)(2,1)}), bf16[32,3,32,512]{3,2,1,0:T(8,128)(2,1)}, u32[]{:S(2)}, u32[]{:S(2)}) %all-to-all-start.4) | async-done | bytes 3145760 | tf_op jit(solution)/shard_map/all_to_all | solution.py:93
  287.1 33.1 %all-gather.2.cloned.1.call-done = bf16[32,64,256]{1,0,2:T(8,128)(2,1)} async-done(((bf16[32,64,64]{1,0,2:T(8,128)(2,1)}), bf16[32,64,256]{1,0,2:T(8,128)(2,1)}) %all-gather.2.cloned.1.call-update) | async-done | bytes 1048592 | tf_op jit(solution)/shard_map/all_gather | solution.py:82
  323.0 7.7 %gather_fusion.2 = bf16[160,64,256]{2,1,0:T(8,128)(2,1)} fusion(bf16[32,64,256]{2,1,0:T(8,128)(2,1)S(1)} %copy.73, s32[1024]{0:T(1024)S(1)} %pad_clamp_fusion.1), kind=kCustom, calls=%fused_computation.2 | custom fusion | bytes 10486400 | tf_op jit(solution)/shard_map/gather | solution.py:99
  330.7 27.6 %all-to-all-done.1 = bf16[32,3,64,512]{3,2,1,0:T(8,128)(2,1)} async-done(((bf16[32,3,64,512]{3,2,1,0:T(8,128)(2,1)}), bf16[32,3,64,512]{3,2,1,0:T(8,128)(2,1)}, u32[]{:S(2)}, u32[]{:S(2)}) %all-to-all-start.1) | async-done | bytes 6291488 | tf_op jit(solution)/shard_map/all_to_all | solution.py:94
  358.3 14.0 %all-to-all-start.3 = ((bf16[32,5,64,256]{3,2,1,0:T(8,128)(2,1)}), bf16[32,5,64,256]{3,2,1,0:T(8,128)(2,1)}, u32[]{:S(2)}, u32[]{:S(2)}) async-start(bf16[32,5,64,256]{3,2,1,0:T(8,128)(2,1)} %bitcast.86), calls=%async_computation.3 | async-start | bytes 10485760 | tf_op jit(solution)/shard_map/all_to_all | solution.py:98
  397.6 5.7 gather_fusion.1
  403.3 8.5 %copy.69 = bf16[32,64,2,512]{3,2,1,0:T(2,128)(2,1)} copy(bf16[32,64,2,512]{3,1,2,0:T(8,128)(2,1)} %bitcast.87) | data formatting | bytes 8388608 | tf_op jit(solution)/shard_map/transpose | solution.py:67
  411.8 7.9 %concatenate.16 = bf16[8,4,64,1024]{3,2,1,0:T(8,128)(2,1)} reshape(bf16[32,64,2,512]{3,2,1,0:T(2,128)(2,1)} %copy.69) | data formatting | bytes 8388608 | tf_op jit(solution)/shard_map/concatenate | solution.py:109
  419.7 17.0 %all-to-all-done.3 = bf16[32,5,64,256]{3,2,1,0:T(8,128)(2,1)} async-done(((bf16[32,5,64,256]{3,2,1,0:T(8,128)(2,1)}), bf16[32,5,64,256]{3,2,1,0:T(8,128)(2,1)}, u32[]{:S(2)}, u32[]{:S(2)}) %all-to-all-start.3) | async-done | bytes 5242912 | tf_op jit(solution)/shard_map/all_to_all | solution.py:98
  436.7 5.2 gather_fusion.3
  441.9 8.1 %copy.75 = bf16[32,64,4,256]{3,2,1,0:T(4,128)(2,1)} copy(bf16[32,64,4,256]{3,1,2,0:T(8,128)(2,1)} %bitcast.88) | data formatting | bytes 8388608 | tf_op jit(solution)/shard_map/transpose | solution.py:67
  450.0 7.8 %concatenate.17 = bf16[8,4,64,1024]{3,2,1,0:T(8,128)(2,1)} reshape(bf16[32,64,4,256]{3,2,1,0:T(4,128)(2,1)} %copy.75) | data formatting | bytes 8388608 | tf_op jit(solution)/shard_map/concatenate | solution.py:109
  457.8 8.2 %pad_maximum_fusion = bf16[8,4,64,2048]{3,2,1,0:T(8,128)(2,1)} fusion(bf16[8,4,64,1024]{3,2,1,0:T(8,128)(2,1)} %concatenate.17, bf16[8,4,64,1024]{3,2,1,0:T(8,128)(2,1)} %concatenate.16), kind=kLoop, calls=%fused_computation.34 | loop fusion | flops 16777216 | bytes 16777216 | tf_op jit(solution)/shard_map/concatenate | solution.py:109
  465.9 146.8 %while.10 = (s32[]{:T(128)}, f32[8,4,64,512]{3,2,1,0:T(8,128)}, bf16[8,4,64,2048]{3,2,1,0:T(8,128)(2,1)}, bf16[8,4,32,512]{3,2,1,0:T(8,128)(2,1)S(1)}, bf16[8,4,32,2048]{3,2,1,0:T(8,128)(2,1)}, /*index=5*/s32[]{:T(128)}) while((s32[]{:T(128)}, f32[8,4,64,512]{3,2,1,0:T(8,128)}, bf16[8,4,64,2048]{3,2,1,0:T(8,128)(2,1)}, ...), condition=%wide.region_9.10_spmd, body=%wide.region_6.9_spmd.sunk | while | flops 3507410944 | bytes 36522060 | solution.py:43
  470.8 13.6 %fusion.45 = f32[8,4,64,512]{3,2,1,0:T(8,128)} fusion(f32[8,4,64,512]{3,2,1,0:T(8,128)} %get-tuple-element.85, s32[]{:T(128)} %get-tuple-element.84, f32[4,512,2048]{2,1,0:T(8,128)S(1)} %fusion.44, f32[4,2048]{1,0:T(4,128)S(1)} %multiply_reduce_fusion.4, f32[4,512]{1,0:T(4,128)S(1)} %multiply_reduce_fusion.5, ...), kind=kOutput, calls=%fused_computation.20.clone.1 | convolution fusion | flops 3238002688 | bytes 18392064 | tf_op jit(solution)/shard_map/while/body/eval_jaxpr/vmap(rm,tm->rt)/dot_general | solution.py:20
  489.2 13.6 %fusion.45 = f32[8,4,64,512]{3,2,1,0:T(8,128)} fusion(f32[8,4,64,512]{3,2,1,0:T(8,128)} %get-tuple-element.85, s32[]{:T(128)} %get-tuple-element.84, f32[4,512,2048]{2,1,0:T(8,128)S(1)} %fusion.44, f32[4,2048]{1,0:T(4,128)S(1)} %multiply_reduce_fusion.4, f32[4,512]{1,0:T(4,128)S(1)} %multiply_reduce_fusion.5, ...), kind=kOutput, calls=%fused_computation.20.clone.1 | convolution fusion | flops 3238002688 | bytes 18392064 | tf_op jit(solution)/shard_map/while/body/eval_jaxpr/vmap(rm,tm->rt)/dot_general | solution.py:20
  507.5 13.6 %fusion.45 = f32[8,4,64,512]{3,2,1,0:T(8,128)} fusion(f32[8,4,64,512]{3,2,1,0:T(8,128)} %get-tuple-element.85, s32[]{:T(128)} %get-tuple-element.84, f32[4,512,2048]{2,1,0:T(8,128)S(1)} %fusion.44, f32[4,2048]{1,0:T(4,128)S(1)} %multiply_reduce_fusion.4, f32[4,512]{1,0:T(4,128)S(1)} %multiply_reduce_fusion.5, ...), kind=kOutput, calls=%fused_computation.20.clone.1 | convolution fusion | flops 3238002688 | bytes 18392064 | tf_op jit(solution)/shard_map/while/body/eval_jaxpr/vmap(rm,tm->rt)/dot_general | solution.py:20
  525.8 13.6 %fusion.45 = f32[8,4,64,512]{3,2,1,0:T(8,128)} fusion(f32[8,4,64,512]{3,2,1,0:T(8,128)} %get-tuple-element.85, s32[]{:T(128)} %get-tuple-element.84, f32[4,512,2048]{2,1,0:T(8,128)S(1)} %fusion.44, f32[4,2048]{1,0:T(4,128)S(1)} %multiply_reduce_fusion.4, f32[4,512]{1,0:T(4,128)S(1)} %multiply_reduce_fusion.5, ...), kind=kOutput, calls=%fused_computation.20.clone.1 | convolution fusion | flops 3238002688 | bytes 18392064 | tf_op jit(solution)/shard_map/while/body/eval_jaxpr/vmap(rm,tm->rt)/dot_general | solution.py:20
  544.1 13.6 %fusion.45 = f32[8,4,64,512]{3,2,1,0:T(8,128)} fusion(f32[8,4,64,512]{3,2,1,0:T(8,128)} %get-tuple-element.85, s32[]{:T(128)} %get-tuple-element.84, f32[4,512,2048]{2,1,0:T(8,128)S(1)} %fusion.44, f32[4,2048]{1,0:T(4,128)S(1)} %multiply_reduce_fusion.4, f32[4,512]{1,0:T(4,128)S(1)} %multiply_reduce_fusion.5, ...), kind=kOutput, calls=%fused_computation.20.clone.1 | convolution fusion | flops 3238002688 | bytes 18392064 | tf_op jit(solution)/shard_map/while/body/eval_jaxpr/vmap(rm,tm->rt)/dot_general | solution.py:20
  562.4 13.6 %fusion.45 = f32[8,4,64,512]{3,2,1,0:T(8,128)} fusion(f32[8,4,64,512]{3,2,1,0:T(8,128)} %get-tuple-element.85, s32[]{:T(128)} %get-tuple-element.84, f32[4,512,2048]{2,1,0:T(8,128)S(1)} %fusion.44, f32[4,2048]{1,0:T(4,128)S(1)} %multiply_reduce_fusion.4, f32[4,512]{1,0:T(4,128)S(1)} %multiply_reduce_fusion.5, ...), kind=kOutput, calls=%fused_computation.20.clone.1 | convolution fusion | flops 3238002688 | bytes 18392064 | tf_op jit(solution)/shard_map/while/body/eval_jaxpr/vmap(rm,tm->rt)/dot_general | solution.py:20
  580.8 13.6 %fusion.45 = f32[8,4,64,512]{3,2,1,0:T(8,128)} fusion(f32[8,4,64,512]{3,2,1,0:T(8,128)} %get-tuple-element.85, s32[]{:T(128)} %get-tuple-element.84, f32[4,512,2048]{2,1,0:T(8,128)S(1)} %fusion.44, f32[4,2048]{1,0:T(4,128)S(1)} %multiply_reduce_fusion.4, f32[4,512]{1,0:T(4,128)S(1)} %multiply_reduce_fusion.5, ...), kind=kOutput, calls=%fused_computation.20.clone.1 | convolution fusion | flops 3238002688 | bytes 18392064 | tf_op jit(solution)/shard_map/while/body/eval_jaxpr/vmap(rm,tm->rt)/dot_general | solution.py:20
  599.1 13.6 %fusion.45 = f32[8,4,64,512]{3,2,1,0:T(8,128)} fusion(f32[8,4,64,512]{3,2,1,0:T(8,128)} %get-tuple-element.85, s32[]{:T(128)} %get-tuple-element.84, f32[4,512,2048]{2,1,0:T(8,128)S(1)} %fusion.44, f32[4,2048]{1,0:T(4,128)S(1)} %multiply_reduce_fusion.4, f32[4,512]{1,0:T(4,128)S(1)} %multiply_reduce_fusion.5, ...), kind=kOutput, calls=%fused_computation.20.clone.1 | convolution fusion | flops 3238002688 | bytes 18392064 | tf_op jit(solution)/shard_map/while/body/eval_jaxpr/vmap(rm,tm->rt)/dot_general | solution.py:20
  612.7 49.5 %reduce-scatter.2.cloned.1.call-done = f32[32,64,128]{2,1,0:T(8,128)} async-done(((f32[32,64,512]{2,1,0:T(8,128)}), f32[32,64,128]{2,1,0:T(8,128)}) %reduce-scatter.2.cloned.1.call-update) | async-done | bytes 1048592 | tf_op jit(solution)/shard_map/reduce_scatter | solution.py:117
  (88 shorter events, 94.8 us)
Async XLA Ops:
  6.5 229.3 %copy-start = (bf16[32,64,512]{2,1,0:T(8,128)(2,1)S(1)}, bf16[32,64,512]{2,1,0:T(8,128)(2,1)}, u32[]{:S(2)}) copy-start(bf16[32,64,512]{2,1,0:T(8,128)(2,1)} %param.9) | copy-start | bytes 6291460
  8.9 153.7 %all-to-all-start.2 = ((s32[32,1,5]{2,1,0:T(1,128)}), s32[32,1,5]{2,1,0:T(1,128)S(1)}, u32[]{:S(2)}, u32[]{:S(2)}) async-start(s32[32,1,5]{2,1,0:T(1,128)} %bitcast.12), calls=%async_computation.2 | async-start | bytes 32768 | tf_op jit(solution)/shard_map/all_to_all | solution.py:90
  162.6 26.4 %all-to-all-start = ((s32[32,1,3]{2,1,0:T(1,128)}), s32[32,1,3]{2,1,0:T(1,128)S(1)}, u32[]{:S(2)}, u32[]{:S(2)}) async-start(s32[32,1,3]{2,1,0:T(1,128)} %bitcast.4), calls=%async_computation | async-start | bytes 32768 | tf_op jit(solution)/shard_map/all_to_all | solution.py:89
  188.9 7.9 %copy-start.2 = (bf16[32,32,512]{2,1,0:T(8,128)(2,1)S(1)}, bf16[32,32,512]{2,1,0:T(8,128)(2,1)}, u32[]{:S(2)}) copy-start(bf16[32,32,512]{2,1,0:T(8,128)(2,1)} %param.8) | copy-start | bytes 3145732
  188.9 41.6 %all-to-all-start.5 = ((bf16[32,5,32,256]{3,2,1,0:T(8,128)(2,1)}), bf16[32,5,32,256]{3,2,1,0:T(8,128)(2,1)}, u32[]{:S(2)}, u32[]{:S(2)}) async-start(bf16[32,5,32,256]{3,2,1,0:T(8,128)(2,1)} %copy.78), calls=%async_computation.5 | async-start | bytes 5242880 | tf_op jit(solution)/shard_map/all_to_all | solution.py:95
  230.5 45.2 %all-to-all-start.4 = ((bf16[32,3,32,512]{3,2,1,0:T(8,128)(2,1)}), bf16[32,3,32,512]{3,2,1,0:T(8,128)(2,1)}, u32[]{:S(2)}, u32[]{:S(2)}) async-start(bf16[32,3,32,512]{3,2,1,0:T(8,128)(2,1)} %bitcast.90), calls=%async_computation.4 | async-start | bytes 6291456 | tf_op jit(solution)/shard_map/all_to_all | solution.py:93
  275.7 82.5 %all-to-all-start.1 = ((bf16[32,3,64,512]{3,2,1,0:T(8,128)(2,1)}), bf16[32,3,64,512]{3,2,1,0:T(8,128)(2,1)}, u32[]{:S(2)}, u32[]{:S(2)}) async-start(bf16[32,3,64,512]{3,2,1,0:T(8,128)(2,1)} %bitcast.85), calls=%async_computation.1 | async-start | bytes 12582912 | tf_op jit(solution)/shard_map/all_to_all | solution.py:94
  280.9 39.3 %all-gather.2.cloned.1.call-start = ((), (), s32[]{:S(2)}) async-start(), calls=%async_computation.7 | async-start | bytes 2621440 | tf_op jit(solution)/shard_map/all_gather | solution.py:82
  358.3 78.4 %all-to-all-start.3 = ((bf16[32,5,64,256]{3,2,1,0:T(8,128)(2,1)}), bf16[32,5,64,256]{3,2,1,0:T(8,128)(2,1)}, u32[]{:S(2)}, u32[]{:S(2)}) async-start(bf16[32,5,64,256]{3,2,1,0:T(8,128)(2,1)} %bitcast.86), calls=%async_computation.3 | async-start | bytes 10485760 | tf_op jit(solution)/shard_map/all_to_all | solution.py:98
  372.3 290.0 %reduce-scatter.2.cloned.1.call-start = ((), (), s32[]{:S(2)}) async-start(), calls=%async_computation.8 | async-start | bytes 5242880 | tf_op jit(solution)/shard_map/reduce_scatter | solution.py:117
  388.9 4.6 copy-start.3
  612.7 49.5 %copy-start.1 = (bf16[32,64,512]{2,1,0:T(8,128)(2,1)S(1)}, bf16[32,64,512]{2,1,0:T(8,128)(2,1)}, u32[]{:S(2)}) copy-start(bf16[32,64,512]{2,1,0:T(8,128)(2,1)} %param.9) | copy-start | bytes 6291460
Sparse Core Ops, SparseCore 0:
  287.2 32.9 all-gather.1
  612.9 49.3 reduce-scatter.1
where the time goes:
time: 679 us; the launch traced here: 669 us
  local copies, waits for them, and re-layouts  246 us (36%)
  waiting for transfers between devices  192 us (28%)
  matrix products  139 us (20%)
  starting transfers between devices  48.5 us (7%)
  other arithmetic  29.4 us (4%)
  between operations  13.9 us (2%)
    gather x1, local copies, waits for them, and re-layouts, per_device(): jnp.take_along_axis(points, skeleton_index[:, None, :], axis=2)  132 us
    dot_general x8, matrix products, kernel_terms(): jnp.einsum('rm,tm->rt', weights.astype(jnp.float32), kernel, precision=la...  109 us
    reduce_scatter x1, waiting for transfers between devices, per_device(): return lax.psum_scatter(terms, 'nbr', scatter_dimension=2, tiled=True)  49.5 us
    all_to_all x1, waiting for transfers between devices, per_device(): lax.all_to_all(points[near_wanted], 'leaf', split_axis=0, concat_axis=0,...  33.9 us
    all_gather x1, waiting for transfers between devices, per_device(): skeleton_charges = lax.all_gather(partial_value, 'nbr', axis=2, tiled=True)  33.1 us
    all_to_all x1, waiting for transfers between devices, per_device(): lax.all_to_all(skeleton_points[far_wanted], 'leaf', split_axis=0, concat_...  31.1 us
    all_to_all x1, waiting for transfers between devices, per_device(): lax.all_to_all(charges[near_wanted], 'leaf', split_axis=0, concat_axis=0,...  27.6 us
    dot_general x8, matrix products, kernel_terms(): jnp.einsum('dt,dm->tm', targets, sources, preferred_element_type=jnp.floa...  27.3 us
  transfers between devices with their start and end apart: 8, of which 6 were waited for; matrix products, arithmetic and copies ran while one was open for 35% of the time, Pallas kernels for 0%

commit v1 on v0

--- a/solution.py
+++ b/solution.py
@@ -79,7 +79,10 @@
     partial_value = jnp.einsum(
         "lrp,lsp->lrs", charges, projection, preferred_element_type=jnp.float32
     ).astype(jnp.bfloat16)
-    skeleton_charges = lax.all_gather(partial_value, "nbr", axis=2, tiled=True)
+    peers = lax.axis_size("nbr")
+    blocks = jnp.stack([partial_value for _ in range(peers)])
+    blocks = lax.all_to_all(blocks, "nbr", split_axis=0, concat_axis=0)
+    skeleton_charges = jnp.concatenate(blocks, axis=2)
     skeleton_points = jnp.take_along_axis(points, skeleton_index[:, None, :], axis=2)
     near_local, near_slots = slot_plan(near_ids, cap_near, groups, leaf_dev)
     far_local, far_slots = slot_plan(far_ids, cap_far, groups, leaf_dev)

time: 679 us -> 702 us (1.034)
  local copies, waits for them, and re-layouts: 246 us -> 259 us
    all_to_all x1, waiting for transfers between devices: 17 us -> 58.5 us  [per_device(): lax.all_to_all(skeleton_charges[far_wanted], 'leaf', split_axis=0, concat...]
    all_gather x1 -> x0, waiting for transfers between devices: 33.1 us -> none  [per_device(): skeleton_charges = lax.all_gather(partial_value, 'nbr', axis=2, tiled=True)]
    all_to_all x1, waiting for transfers between devices: 33.9 us -> 19.3 us  [per_device(): lax.all_to_all(points[near_wanted], 'leaf', split_axis=0, concat_axis=0,...]
    all_to_all x1, starting transfers between devices: 14 us -> 5.25 us  [per_device(): lax.all_to_all(skeleton_charges[far_wanted], 'leaf', split_axis=0, concat...]
    reshape x0 -> x2, local copies, waits for them, and re-layouts: none -> 8.33 us  [per_device(): skeleton_charges = jnp.concatenate(blocks, axis=2)]
    reduce_sum x8, other arithmetic: 0.45 us -> 7.66 us  [kernel_terms(): jnp.sum(target_f32 * target_f32, axis=0)[:, None]]
    unnamed x12 -> x16, local copies, waits for them, and re-layouts: 6.29 us -> 13.5 us
  transfers between devices with their start and end apart: 8 -> 8, of which waited for: 6 -> 6; matrix products, arithmetic and copies ran while one was open for 35% -> 36% of each run, Pallas kernels for 0% -> 0%
where the time goes in v1:
time: 702 us; the launch traced here: 692 us
  local copies, waits for them, and re-layouts  259 us (37%)
  waiting for transfers between devices  196 us (28%)
  matrix products  140 us (20%)
  starting transfers between devices  48.2 us (7%)
  other arithmetic  35.1 us (5%)
  between operations  13.9 us (2%)
    gather x1, local copies, waits for them, and re-layouts, per_device(): jnp.take_along_axis(points, skeleton_index[:, None, :], axis=2)  132 us
    dot_general x8, matrix products, kernel_terms(): jnp.einsum('rm,tm->rt', weights.astype(jnp.float32), kernel, precision=la...  109 us
    all_to_all x1, waiting for transfers between devices, per_device(): lax.all_to_all(skeleton_charges[far_wanted], 'leaf', split_axis=0, concat...  58.5 us
    reduce_scatter x1, waiting for transfers between devices, per_device(): return lax.psum_scatter(terms, 'nbr', scatter_dimension=2, tiled=True)  54.9 us
    all_to_all x1, waiting for transfers between devices, per_device(): lax.all_to_all(skeleton_points[far_wanted], 'leaf', split_axis=0, concat_...  31.1 us
    all_to_all x1, waiting for transfers between devices, per_device(): lax.all_to_all(charges[near_wanted], 'leaf', split_axis=0, concat_axis=0,...  30.5 us
    dot_general x8, matrix products, kernel_terms(): jnp.einsum('dt,dm->tm', targets, sources, preferred_element_type=jnp.floa...  27.9 us
    transpose x4, local copies, waits for them, and re-layouts, gather_entries(): picked.transpose(0, 2, 1, 3)  23.5 us
  transfers between devices with their start and end apart: 8, of which 6 were waited for; matrix products, arithmetic and copies ran while one was open for 36% of the time, Pallas kernels for 0%

profile of v1, /device:TPU:1, one launch (start us, length us, event | category | flops | bytes accessed | tf_op | source)
XLA Modules:
  0.0 692.3 jit_solution(3236454011176533825)
XLA Ops:
  8.8 8.6 %all-to-all-start = ((s32[32,1,3]{2,1,0:T(1,128)}), s32[32,1,3]{2,1,0:T(1,128)S(1)}, u32[]{:S(2)}, u32[]{:S(2)}) async-start(s32[32,1,3]{2,1,0:T(1,128)} %bitcast.4), calls=%async_computation | async-start | bytes 32768 | tf_op jit(solution)/shard_map/all_to_all | solution.py:92
  24.3 5.8 all-to-all-start.3
  40.5 132.5 %gather_fusion.8 = bf16[8192,32]{1,0:T(8,128)(2,1)} fusion(bf16[32,32,512]{1,2,0:T(8,128)(2,1)} %copy.60, s32[8192]{0:T(1024)S(1)} %bitcast.84), kind=kCustom, calls=%fused_computation.8 | custom fusion | bytes 1114112 | tf_op jit(solution)/shard_map/jit(take_along_axis)/gather | solution.py:86
  182.6 9.2 %gather_fusion.6 = bf16[160,32,256]{1,2,0:T(8,128)(2,1)} fusion(bf16[32,32,256]{1,2,0:T(8,128)(2,1)} %select_bitcast_fusion, s32[1024]{0:T(1024)S(1)} %pad_clamp_fusion.1), kind=kCustom, calls=%fused_computation.6 | custom fusion | bytes 5243520 | tf_op jit(solution)/shard_map/gather | solution.py:99
  191.8 9.8 %copy.61 = bf16[32,5,32,256]{3,2,1,0:T(8,128)(2,1)} copy(bf16[32,5,32,256]{2,3,1,0:T(8,128)(2,1)} %bitcast.90) | data formatting | bytes 5242880 | tf_op jit(solution)/shard_map/gather | solution.py:99
  201.6 7.6 %all-to-all-start.6 = ((bf16[32,5,32,256]{3,2,1,0:T(8,128)(2,1)}), bf16[32,5,32,256]{3,2,1,0:T(8,128)(2,1)}, u32[]{:S(2)}, u32[]{:S(2)}) async-start(bf16[32,5,32,256]{3,2,1,0:T(8,128)(2,1)} %copy.61), calls=%async_computation.6 | async-start | bytes 5242880 | tf_op jit(solution)/shard_map/all_to_all | solution.py:98
  212.1 31.1 %all-to-all-done.6 = bf16[32,5,32,256]{3,2,1,0:T(8,128)(2,1)} async-done(((bf16[32,5,32,256]{3,2,1,0:T(8,128)(2,1)}), bf16[32,5,32,256]{3,2,1,0:T(8,128)(2,1)}, u32[]{:S(2)}, u32[]{:S(2)}) %all-to-all-start.6) | async-done | bytes 2621472 | tf_op jit(solution)/shard_map/all_to_all | solution.py:98
  243.2 5.8 all-to-all-start.5
  261.6 7.7 %gather_fusion.2 = bf16[160,64,256]{2,1,0:T(8,128)(2,1)} fusion(bf16[32,64,256]{2,1,0:T(8,128)(2,1)S(1)} %reshape.413, s32[1024]{0:T(1024)S(1)} %pad_clamp_fusion.1), kind=kCustom, calls=%fused_computation.2 | custom fusion | bytes 10486400 | tf_op jit(solution)/shard_map/gather | solution.py:102
  269.3 19.3 %all-to-all-done.5 = bf16[32,3,32,512]{3,2,1,0:T(8,128)(2,1)} async-done(((bf16[32,3,32,512]{3,2,1,0:T(8,128)(2,1)}), bf16[32,3,32,512]{3,2,1,0:T(8,128)(2,1)}, u32[]{:S(2)}, u32[]{:S(2)}) %all-to-all-start.5) | async-done | bytes 3145760 | tf_op jit(solution)/shard_map/all_to_all | solution.py:96
  288.6 5.2 all-to-all-start.4
  293.9 6.0 gather_fusion
  299.9 58.5 %all-to-all-done.4 = bf16[32,5,64,256]{3,2,1,0:T(8,128)(2,1)} async-done(((bf16[32,5,64,256]{3,2,1,0:T(8,128)(2,1)}), bf16[32,5,64,256]{3,2,1,0:T(8,128)(2,1)}, u32[]{:S(2)}, u32[]{:S(2)}) %all-to-all-start.4) | async-done | bytes 5242912 | tf_op jit(solution)/shard_map/all_to_all | solution.py:101
  358.4 9.6 %all-to-all-start.1 = ((bf16[32,3,64,512]{3,2,1,0:T(8,128)(2,1)}), bf16[32,3,64,512]{3,2,1,0:T(8,128)(2,1)}, u32[]{:S(2)}, u32[]{:S(2)}) async-start(bf16[32,3,64,512]{3,2,1,0:T(8,128)(2,1)} %bitcast.86), calls=%async_computation.1 | async-start | bytes 12582912 | tf_op jit(solution)/shard_map/all_to_all | solution.py:97
  393.9 5.4 gather_fusion.3
  399.3 8.1 %copy.58 = bf16[32,64,4,256]{3,2,1,0:T(4,128)(2,1)} copy(bf16[32,64,4,256]{3,1,2,0:T(8,128)(2,1)} %bitcast.88) | data formatting | bytes 8388608 | tf_op jit(solution)/shard_map/transpose | solution.py:67
  407.4 7.9 %concatenate.17 = bf16[8,4,64,1024]{3,2,1,0:T(8,128)(2,1)} reshape(bf16[32,64,4,256]{3,2,1,0:T(4,128)(2,1)} %copy.58) | data formatting | bytes 8388608 | tf_op jit(solution)/shard_map/concatenate | solution.py:112
  415.3 30.5 %all-to-all-done.1 = bf16[32,3,64,512]{3,2,1,0:T(8,128)(2,1)} async-done(((bf16[32,3,64,512]{3,2,1,0:T(8,128)(2,1)}), bf16[32,3,64,512]{3,2,1,0:T(8,128)(2,1)}, u32[]{:S(2)}, u32[]{:S(2)}) %all-to-all-start.1) | async-done | bytes 6291488 | tf_op jit(solution)/shard_map/all_to_all | solution.py:97
  445.8 5.6 gather_fusion.1
  451.4 8.5 %copy.53 = bf16[32,64,2,512]{3,2,1,0:T(2,128)(2,1)} copy(bf16[32,64,2,512]{3,1,2,0:T(8,128)(2,1)} %bitcast.89) | data formatting | bytes 8388608 | tf_op jit(solution)/shard_map/transpose | solution.py:67
  459.9 7.8 %concatenate.16 = bf16[8,4,64,1024]{3,2,1,0:T(8,128)(2,1)} reshape(bf16[32,64,2,512]{3,2,1,0:T(2,128)(2,1)} %copy.53) | data formatting | bytes 8388608 | tf_op jit(solution)/shard_map/concatenate | solution.py:112
  467.6 8.2 %pad_maximum_fusion = bf16[8,4,64,2048]{3,2,1,0:T(8,128)(2,1)} fusion(bf16[8,4,64,1024]{3,2,1,0:T(8,128)(2,1)} %concatenate.17, bf16[8,4,64,1024]{3,2,1,0:T(8,128)(2,1)} %concatenate.16), kind=kLoop, calls=%fused_computation.34 | loop fusion | flops 16777216 | bytes 16777216 | tf_op jit(solution)/shard_map/concatenate | solution.py:112
  475.8 154.6 %while.10 = (s32[]{:T(128)}, f32[8,4,64,512]{3,2,1,0:T(8,128)}, bf16[8,4,64,2048]{3,2,1,0:T(8,128)(2,1)}, bf16[8,4,32,512]{3,2,1,0:T(8,128)(2,1)}, bf16[8,4,32,2048]{3,2,1,0:T(8,128)(2,1)}, /*index=5*/s32[]{:T(128)}) while((s32[]{:T(128)}, f32[8,4,64,512]{3,2,1,0:T(8,128)}, bf16[8,4,64,2048]{3,2,1,0:T(8,128)(2,1)}, ...), condition=%wide.region_9.10_spmd, body=%wide.region_6.9_spmd.sunk | while | flops 3507410944 | bytes 36522060 | solution.py:43
  481.6 13.6 %fusion.45 = f32[8,4,64,512]{3,2,1,0:T(8,128)} fusion(f32[8,4,64,512]{3,2,1,0:T(8,128)} %get-tuple-element.85, s32[]{:T(128)} %get-tuple-element.84, f32[4,512,2048]{2,1,0:T(8,128)S(1)} %fusion.44, f32[4,2048]{1,0:T(4,128)S(1)} %multiply_reduce_fusion.4, f32[4,512]{1,0:T(4,128)S(1)} %multiply_reduce_fusion.5, ...), kind=kOutput, calls=%fused_computation.20.clone.1 | convolution fusion | flops 3238002688 | bytes 18392064 | tf_op jit(solution)/shard_map/while/body/eval_jaxpr/vmap(rm,tm->rt)/dot_general | solution.py:20
  501.0 13.6 %fusion.45 = f32[8,4,64,512]{3,2,1,0:T(8,128)} fusion(f32[8,4,64,512]{3,2,1,0:T(8,128)} %get-tuple-element.85, s32[]{:T(128)} %get-tuple-element.84, f32[4,512,2048]{2,1,0:T(8,128)S(1)} %fusion.44, f32[4,2048]{1,0:T(4,128)S(1)} %multiply_reduce_fusion.4, f32[4,512]{1,0:T(4,128)S(1)} %multiply_reduce_fusion.5, ...), kind=kOutput, calls=%fused_computation.20.clone.1 | convolution fusion | flops 3238002688 | bytes 18392064 | tf_op jit(solution)/shard_map/while/body/eval_jaxpr/vmap(rm,tm->rt)/dot_general | solution.py:20
  520.2 13.6 %fusion.45 = f32[8,4,64,512]{3,2,1,0:T(8,128)} fusion(f32[8,4,64,512]{3,2,1,0:T(8,128)} %get-tuple-element.85, s32[]{:T(128)} %get-tuple-element.84, f32[4,512,2048]{2,1,0:T(8,128)S(1)} %fusion.44, f32[4,2048]{1,0:T(4,128)S(1)} %multiply_reduce_fusion.4, f32[4,512]{1,0:T(4,128)S(1)} %multiply_reduce_fusion.5, ...), kind=kOutput, calls=%fused_computation.20.clone.1 | convolution fusion | flops 3238002688 | bytes 18392064 | tf_op jit(solution)/shard_map/while/body/eval_jaxpr/vmap(rm,tm->rt)/dot_general | solution.py:20
  539.5 13.6 %fusion.45 = f32[8,4,64,512]{3,2,1,0:T(8,128)} fusion(f32[8,4,64,512]{3,2,1,0:T(8,128)} %get-tuple-element.85, s32[]{:T(128)} %get-tuple-element.84, f32[4,512,2048]{2,1,0:T(8,128)S(1)} %fusion.44, f32[4,2048]{1,0:T(4,128)S(1)} %multiply_reduce_fusion.4, f32[4,512]{1,0:T(4,128)S(1)} %multiply_reduce_fusion.5, ...), kind=kOutput, calls=%fused_computation.20.clone.1 | convolution fusion | flops 3238002688 | bytes 18392064 | tf_op jit(solution)/shard_map/while/body/eval_jaxpr/vmap(rm,tm->rt)/dot_general | solution.py:20
  558.8 13.6 %fusion.45 = f32[8,4,64,512]{3,2,1,0:T(8,128)} fusion(f32[8,4,64,512]{3,2,1,0:T(8,128)} %get-tuple-element.85, s32[]{:T(128)} %get-tuple-element.84, f32[4,512,2048]{2,1,0:T(8,128)S(1)} %fusion.44, f32[4,2048]{1,0:T(4,128)S(1)} %multiply_reduce_fusion.4, f32[4,512]{1,0:T(4,128)S(1)} %multiply_reduce_fusion.5, ...), kind=kOutput, calls=%fused_computation.20.clone.1 | convolution fusion | flops 3238002688 | bytes 18392064 | tf_op jit(solution)/shard_map/while/body/eval_jaxpr/vmap(rm,tm->rt)/dot_general | solution.py:20
  578.1 13.6 %fusion.45 = f32[8,4,64,512]{3,2,1,0:T(8,128)} fusion(f32[8,4,64,512]{3,2,1,0:T(8,128)} %get-tuple-element.85, s32[]{:T(128)} %get-tuple-element.84, f32[4,512,2048]{2,1,0:T(8,128)S(1)} %fusion.44, f32[4,2048]{1,0:T(4,128)S(1)} %multiply_reduce_fusion.4, f32[4,512]{1,0:T(4,128)S(1)} %multiply_reduce_fusion.5, ...), kind=kOutput, calls=%fused_computation.20.clone.1 | convolution fusion | flops 3238002688 | bytes 18392064 | tf_op jit(solution)/shard_map/while/body/eval_jaxpr/vmap(rm,tm->rt)/dot_general | solution.py:20
  597.4 13.6 %fusion.45 = f32[8,4,64,512]{3,2,1,0:T(8,128)} fusion(f32[8,4,64,512]{3,2,1,0:T(8,128)} %get-tuple-element.85, s32[]{:T(128)} %get-tuple-element.84, f32[4,512,2048]{2,1,0:T(8,128)S(1)} %fusion.44, f32[4,2048]{1,0:T(4,128)S(1)} %multiply_reduce_fusion.4, f32[4,512]{1,0:T(4,128)S(1)} %multiply_reduce_fusion.5, ...), kind=kOutput, calls=%fused_computation.20.clone.1 | convolution fusion | flops 3238002688 | bytes 18392064 | tf_op jit(solution)/shard_map/while/body/eval_jaxpr/vmap(rm,tm->rt)/dot_general | solution.py:20
  616.7 13.6 %fusion.45 = f32[8,4,64,512]{3,2,1,0:T(8,128)} fusion(f32[8,4,64,512]{3,2,1,0:T(8,128)} %get-tuple-element.85, s32[]{:T(128)} %get-tuple-element.84, f32[4,512,2048]{2,1,0:T(8,128)S(1)} %fusion.44, f32[4,2048]{1,0:T(4,128)S(1)} %multiply_reduce_fusion.4, f32[4,512]{1,0:T(4,128)S(1)} %multiply_reduce_fusion.5, ...), kind=kOutput, calls=%fused_computation.20.clone.1 | convolution fusion | flops 3238002688 | bytes 18392064 | tf_op jit(solution)/shard_map/while/body/eval_jaxpr/vmap(rm,tm->rt)/dot_general | solution.py:20
  630.4 54.9 %reduce-scatter.2.cloned.1.call-done = f32[32,64,128]{2,1,0:T(8,128)} async-done(((f32[32,64,512]{2,1,0:T(8,128)}), f32[32,64,128]{2,1,0:T(8,128)}) %reduce-scatter.2.cloned.1.call-update) | async-done | bytes 1048592 | tf_op jit(solution)/shard_map/reduce_scatter | solution.py:120
  (92 shorter events, 115.7 us)
Async XLA Ops:
  6.5 12.1 %copy-start = (bf16[32,64,512]{2,1,0:T(8,128)(2,1)S(1)}, bf16[32,64,512]{2,1,0:T(8,128)(2,1)}, u32[]{:S(2)}) copy-start(bf16[32,64,512]{2,1,0:T(8,128)(2,1)} %param.9) | copy-start | bytes 6291460
  6.5 23.5 %copy-start.4 = (s32[32,256]{1,0:T(8,128)S(1)}, s32[32,256]{1,0:T(8,128)}, u32[]{:S(2)}) copy-start(s32[32,256]{1,0:T(8,128)} %param.11) | copy-start | bytes 98308
  8.8 15.6 %all-to-all-start = ((s32[32,1,3]{2,1,0:T(1,128)}), s32[32,1,3]{2,1,0:T(1,128)S(1)}, u32[]{:S(2)}, u32[]{:S(2)}) async-start(s32[32,1,3]{2,1,0:T(1,128)} %bitcast.4), calls=%async_computation | async-start | bytes 32768 | tf_op jit(solution)/shard_map/all_to_all | solution.py:92
  18.7 18.7 %copy-start.2 = (bf16[32,32,512]{2,1,0:T(8,128)(2,1)S(1)}, bf16[32,32,512]{2,1,0:T(8,128)(2,1)}, u32[]{:S(2)}) copy-start(bf16[32,32,512]{2,1,0:T(8,128)(2,1)} %param.8) | copy-start | bytes 3145732
  24.3 148.7 %all-to-all-start.3 = ((s32[32,1,5]{2,1,0:T(1,128)}), s32[32,1,5]{2,1,0:T(1,128)S(1)}, u32[]{:S(2)}, u32[]{:S(2)}) async-start(s32[32,1,5]{2,1,0:T(1,128)} %bitcast.13), calls=%async_computation.3 | async-start | bytes 32768 | tf_op jit(solution)/shard_map/all_to_all | solution.py:93
  173.0 28.6 %all-to-all-start.2 = ((bf16[4,2,65536]{2,1,0:T(2,128)(2,1)}), bf16[4,2,65536]{2,1,0:T(2,128)(2,1)}, u32[]{:S(2)}, u32[]{:S(2)}) async-start(bf16[4,2,65536]{2,1,0:T(2,128)(2,1)} %reshape.504), calls=%async_computation.2 | async-start | bytes 2097152 | tf_op jit(solution)/shard_map/all_to_all | solution.py:84
  201.6 41.6 %all-to-all-start.6 = ((bf16[32,5,32,256]{3,2,1,0:T(8,128)(2,1)}), bf16[32,5,32,256]{3,2,1,0:T(8,128)(2,1)}, u32[]{:S(2)}, u32[]{:S(2)}) async-start(bf16[32,5,32,256]{3,2,1,0:T(8,128)(2,1)} %copy.61), calls=%async_computation.6 | async-start | bytes 5242880 | tf_op jit(solution)/shard_map/all_to_all | solution.py:98
  243.2 45.4 %all-to-all-start.5 = ((bf16[32,3,32,512]{3,2,1,0:T(8,128)(2,1)}), bf16[32,3,32,512]{3,2,1,0:T(8,128)(2,1)}, u32[]{:S(2)}, u32[]{:S(2)}) async-start(bf16[32,3,32,512]{3,2,1,0:T(8,128)(2,1)} %bitcast.91), calls=%async_computation.5 | async-start | bytes 6291456 | tf_op jit(solution)/shard_map/all_to_all | solution.py:96
  288.6 69.8 %all-to-all-start.4 = ((bf16[32,5,64,256]{3,2,1,0:T(8,128)(2,1)}), bf16[32,5,64,256]{3,2,1,0:T(8,128)(2,1)}, u32[]{:S(2)}, u32[]{:S(2)}) async-start(bf16[32,5,64,256]{3,2,1,0:T(8,128)(2,1)} %bitcast.87), calls=%async_computation.4 | async-start | bytes 10485760 | tf_op jit(solution)/shard_map/all_to_all | solution.py:101
  358.4 87.4 %all-to-all-start.1 = ((bf16[32,3,64,512]{3,2,1,0:T(8,128)(2,1)}), bf16[32,3,64,512]{3,2,1,0:T(8,128)(2,1)}, u32[]{:S(2)}, u32[]{:S(2)}) async-start(bf16[32,3,64,512]{3,2,1,0:T(8,128)(2,1)} %bitcast.86), calls=%async_computation.1 | async-start | bytes 12582912 | tf_op jit(solution)/shard_map/all_to_all | solution.py:97
  368.0 317.2 %reduce-scatter.2.cloned.1.call-start = ((), (), s32[]{:S(2)}) async-start(), calls=%async_computation.8 | async-start | bytes 5242880 | tf_op jit(solution)/shard_map/reduce_scatter | solution.py:120
  385.2 4.6 copy-start.3
  630.3 54.9 %copy-start.1 = (bf16[32,64,512]{2,1,0:T(8,128)(2,1)S(1)}, bf16[32,64,512]{2,1,0:T(8,128)(2,1)}, u32[]{:S(2)}) copy-start(bf16[32,64,512]{2,1,0:T(8,128)(2,1)} %param.9) | copy-start | bytes 6291460
Sparse Core Ops, SparseCore 0:
  630.5 54.7 reduce-scatter.1
